TPU v7x, 16 devices: a whole 2x2x2 slice. The times are simulated.
16 devices in a mesh: dp: 1, tp: 16 (over x, y, z, core).
Axes of the slice: x: 2, y: 2, z: 2, core: 2. Of those that a mesh axis runs over, the one named last changes fastest.
Arguments:
- x: bfloat16 [2048, 5120], P('dp')
- dy: bfloat16 [2048, 5120], P('dp')
- gate: bfloat16 [2048, 12288], P('dp', 'tp')
- up: bfloat16 [2048, 12288], P('dp', 'tp')
- w_gate: bfloat16 [5120, 12288], P(None, 'tp')
- w_up: bfloat16 [5120, 12288], P(None, 'tp')
- w_down: bfloat16 [12288, 5120], P('tp')
Outputs:
- output 1: bfloat16 [2048, 5120], P('dp')
- output 2: bfloat16 [5120, 12288], P('dp', 'tp')
- output 3: bfloat16 [5120, 12288], P('dp', 'tp')
- output 4: bfloat16 [12288, 5120], P(('dp', 'tp'))
All inputs are finite; a program needn't handle non-finite values.
Results may differ from a plain program's by a relative error of at most 0.012.
Values are sent between devices in bfloat16 or wider.
A program may use at most 2 GiB of HBM per device.

v0:
```python
import functools

import jax
import jax.numpy as jnp
from jax import lax
from jax.experimental import pallas as pl
from jax.experimental.pallas import tpu as pltpu
from jax.sharding import PartitionSpec as P

MESH = pl.DeviceIdType.MESH
BF, F32 = jnp.bfloat16, jnp.float32
NT = (((1,), (1,)), ((), ()))
TN = (((0,), (0,)), ((), ()))
NN = (((1,), (0,)), ((), ()))
NG = 8
ORDERS = ((8, 4, 2), (4, 2, 8), (2, 8, 4))


def dot(a, b, dims):
    return lax.dot_general(a, b, dims, preferred_element_type=F32)


def colours(half):
    tiles = half // 128
    widths = [128 * ((tiles + 2 - k) // 3) for k in range(3)]
    return [(sum(widths[:k]), widths[k]) for k in range(3)]


def kernel(
    x, dy, gate, up, w_gate, w_up, w_down,
    dx, dw_gate, dw_up, dw_down,
    d_all, hid_t, acc0, acc1, acc2, acc3, d2d_out, d2d_in, out1, out2, out3, in1, in2, in3, fin,
    load, d2d_s, d2d_r, s1, s2, s3, r1, r2, r3, a_loc, a3s, a3r, a2s, a2r, a1s, a1r, ds, dr, credit, st,
    *, cb,
):
    rows, wide = x.shape
    ff = gate.shape[1]
    g_rows, half = rows // NG, wide // 2
    cols = colours(half)
    steps = wide // cb
    me = lax.axis_index("tp")
    core = lax.rem(me, 2)
    sib = me + 1 - 2 * core
    mine = pl.multiple_of(core * half, 128)
    other = pl.multiple_of((1 - core) * half, 128)

    def bit(stride):
        return lax.rem(me // stride, 2)

    def peer(stride):
        return me + (1 - 2 * bit(stride)) * stride

    def rows_at(start, size):
        return pl.ds(pl.multiple_of(start, size), size)

    def remote(src, dst, send, recv, to):
        return pltpu.make_async_remote_copy(
            src_ref=src, dst_ref=dst, send_sem=send, recv_sem=recv,
            device_id={"tp": to}, device_id_type=MESH,
        )

    def c_d2d():
        return remote(d2d_out, d2d_in, d2d_s, d2d_r, sib)

    def c_rs(stage, g, k):
        src, dst, send, recv = ((out1, in1, s1, r1), (out2, in2, s2, r2), (out3, in3, s3, r3))[stage]
        c = pl.ds(*cols[k])
        return remote(src.at[:, c], dst.at[g, :, c], send.at[k], recv.at[k, g], peer(ORDERS[k][stage]))

    def region(g, k, depth):
        start, size = g * g_rows, g_rows
        for stage in range(depth):
            size //= 2
            start = start + bit(ORDERS[k][stage]) * size
        return dx.at[rows_at(start, size), pl.ds(pl.multiple_of(mine + cols[k][0], 128), cols[k][1])]

    def c_local(g, k):
        return pltpu.make_async_copy(fin.at[g, :, pl.ds(*cols[k])], region(g, k, 3), a_loc.at[k, g])

    def c_a0(g, k):
        return remote(fin.at[g, :, pl.ds(*cols[k])], region(g, k, 3), a3s.at[k, g], a3r.at[k, g], peer(ORDERS[k][2]))

    def c_a1(g, k):
        return remote(region(g, k, 2), region(g, k, 2), a2s.at[k, g], a2r.at[k, g], peer(ORDERS[k][1]))

    def c_a2(g, k):
        return remote(region(g, k, 1), region(g, k, 1), a1s.at[k, g], a1r.at[k, g], peer(ORDERS[k][0]))

    def c_a3(g, k):
        return remote(region(g, k, 0), region(g, k, 0), ds.at[k, g], dr.at[k, g], sib)

    def e1(g):
        c_d2d().wait_recv()
        h = g_rows // 2
        for k in range(3):
            c = pl.ds(*cols[k])
            away = rows_at((1 - bit(ORDERS[k][0])) * h, h)

            @pl.when(g > 0)
            def _():
                c_rs(0, g, k).wait_send()

            out1[:, c] = (acc0[away, c] + d2d_in[away, c].astype(F32)).astype(BF)
            c_rs(0, g, k).start()
        for k in range(3):
            c = pl.ds(*cols[k])
            keep = rows_at(bit(ORDERS[k][0]) * h, h)
            acc1[:, c] = acc0[keep, c] + d2d_in[keep, c].astype(F32)

        @pl.when(g < NG - 1)
        def _():
            pl.semaphore_signal(credit, inc=1, device_id={"tp": sib}, device_id_type=MESH)

    def e_mid(stage, g, src, came, out, dst):
        h = src.shape[0] // 2
        for k in range(3):
            c = pl.ds(*cols[k])
            c_rs(stage - 1, g, k).wait_recv()
            away = rows_at((1 - bit(ORDERS[k][stage])) * h, h)

            @pl.when(g > 0)
            def _():
                c_rs(stage, g, k).wait_send()

            out[:, c] = (src[away, c] + came[g, away, c].astype(F32)).astype(BF)
            c_rs(stage, g, k).start()
            keep = rows_at(bit(ORDERS[k][stage]) * h, h)
            dst[:, c] = src[keep, c] + came[g, keep, c].astype(F32)

    def e4(g):
        for k in range(3):
            c = pl.ds(*cols[k])
            c_rs(2, g, k).wait_recv()
            fin[g, :, c] = (acc3[:, c] + in3[g, :, c].astype(F32)).astype(BF)
            c_local(g, k).start()

    def a0(g):
        for k in range(3):
            c_a0(g, k).start()

    def at(cond, f, g):
        @pl.when(cond)
        def _():
            f(g)

    def reduce_events(t):
        at((t >= 3) & (t < NG + 3), e4, t - 3)
        at((t >= 2) & (t < NG + 2), lambda g: e_mid(2, g, acc2, in2, out3, acc3), t - 2)
        at((t >= 1) & (t < NG + 1), lambda g: e_mid(1, g, acc1, in1, out2, acc2), t - 1)

    def a1(g):
        for k in range(3):
            c_local(g, k).wait()
            c_a0(g, k).wait_recv()
            c_a1(g, k).start()

    def a2(g):
        for k in range(3):
            c_a1(g, k).wait_recv()
            c_a2(g, k).start()

    def a3(g):
        for k in range(3):
            c_a2(g, k).wait_recv()
            c_a3(g, k).start()

    def slot(s):
        @pl.when(s < 3)
        def _():
            reduce_events(NG + s)
            at(s >= 0, a0, NG + s - 3)

        for lag, f in ((5, a3), (3, a2), (1, a1)):
            t = s - lag
            g = lax.div(2 * jnp.maximum(t, 0), 5)
            at((t >= 0) & (lax.rem(2 * jnp.maximum(t, 0), 5) < 2) & (g < NG), f, g)

    last_slot = 5 + (5 * (NG - 1) + 1) // 2

    barrier = pltpu.get_barrier_semaphore()
    for to in (sib, peer(8), peer(4), peer(2)):
        pl.semaphore_signal(barrier, inc=1, device_id={"tp": to}, device_id_type=MESH)
    pl.semaphore_wait(barrier, 4)

    def first_phase(wd, wg, wu, dyb, gb, ub):
        def rows_of(g):
            r = rows_at(g * g_rows, g_rows)
            return (
                pltpu.make_async_copy(dy.at[r], dyb, load.at[0]),
                pltpu.make_async_copy(gate.at[r], gb, load.at[1]),
                pltpu.make_async_copy(up.at[r], ub, load.at[2]),
            )

        weights = [pltpu.make_async_copy(a, b, load.at[3 + i]) for i, (a, b) in enumerate(((w_down, wd), (w_gate, wg), (w_up, wu)))]
        weights[0].start()
        for c in rows_of(0):
            c.start()
        weights[1].start()
        weights[2].start()
        weights[0].wait()

        def body(g, _):
            for c in rows_of(g):
                c.wait()
            d_h = dot(dyb[...], wd[...], NT)
            gf, uf = gb[...].astype(F32), ub[...].astype(F32)
            sig = jax.nn.sigmoid(gf)
            silu = gf * sig
            r = rows_at(g * g_rows, g_rows)
            d_all[r, pl.ds(0, ff)] = (d_h * uf * (sig + silu * (1 - sig))).astype(BF)
            d_all[r, pl.ds(ff, ff)] = (d_h * silu).astype(BF)
            hid_t[:, r] = (silu * uf).astype(BF).T

            @pl.when(g < NG - 1)
            def _():
                for c in rows_of(jnp.minimum(g + 1, NG - 1)):
                    c.start()

            @pl.when(g == 0)
            def _():
                weights[1].wait()
                weights[2].wait()

            dg, du = d_all[r, pl.ds(0, ff)], d_all[r, pl.ds(ff, ff)]

            def term(start):
                w = pl.ds(start, half)
                return dot(dg, wg[w, :], NT) + dot(du, wu[w, :], NT)

            @pl.when(g > 0)
            def _():
                c_d2d().wait_send()

            d2d_out[...] = term(other).astype(BF)

            @pl.when(g > 0)
            def _():
                pl.semaphore_wait(credit, 1)

            c_d2d().start()
            acc0[...] = term(mine)
            reduce_events(g)
            e1(g)
            return 0

        lax.fori_loop(0, NG, body, 0)

    pl.run_scoped(
        first_phase,
        pltpu.VMEM((ff, wide), BF),
        pltpu.VMEM((wide, ff), BF),
        pltpu.VMEM((wide, ff), BF),
        pltpu.VMEM((g_rows, wide), BF),
        pltpu.VMEM((g_rows, ff), BF),
        pltpu.VMEM((g_rows, ff), BF),
    )

    def second_phase(xb, yb, og, od):
        def loads(i, b):
            c = rows_at(i * cb, cb)
            return (
                pltpu.make_async_copy(x.at[:, c], xb.at[b], load.at[b]),
                pltpu.make_async_copy(dy.at[:, c], yb.at[b], load.at[2 + b]),
            )

        def stores(i, b):
            c = rows_at(i * cb, cb)
            return (
                pltpu.make_async_copy(og.at[b, :, pl.ds(0, ff)], dw_gate.at[c], st.at[b, 0]),
                pltpu.make_async_copy(og.at[b, :, pl.ds(ff, ff)], dw_up.at[c], st.at[b, 1]),
                pltpu.make_async_copy(od.at[b], dw_down.at[:, c], st.at[b, 2]),
            )

        for c in loads(0, 0):
            c.start()

        def early(g, _):
            a0(g)
            return 0

        lax.fori_loop(0, NG - 3, early, 0)

        def body(i, _):
            b = lax.rem(i, 2)

            @pl.when(i < steps - 1)
            def _():
                for c in loads(jnp.minimum(i + 1, steps - 1), 1 - b):
                    c.start()

            into = loads(i, b)
            out = stores(i, b)

            @pl.when(i >= 2)
            def _():
                for c in out:
                    c.wait()

            into[0].wait()
            og[b] = dot(xb[b], d_all[...], TN).astype(BF)
            out[0].start()
            out[1].start()
            slot(2 * i)
            into[1].wait()
            od[b] = dot(hid_t[...], yb[b], NN).astype(BF)
            out[2].start()
            slot(2 * i + 1)
            return 0

        lax.fori_loop(0, steps, body, 0)

        for i in (steps - 2, steps - 1):
            for c in stores(i, i % 2):
                c.wait()

    pl.run_scoped(
        second_phase,
        pltpu.VMEM((2, rows, cb), BF),
        pltpu.VMEM((2, rows, cb), BF),
        pltpu.VMEM((2, cb, 2 * ff), BF),
        pltpu.VMEM((2, ff, cb), BF),
    )

    def rest(s, _):
        slot(s)
        return 0

    lax.fori_loop(2 * steps, last_slot + 1, rest, 0)

    for k in range(3):
        for stage in range(3):
            c_rs(stage, NG - 1, k).wait_send()
    c_d2d().wait_send()

    def drain(g, _):
        for k in range(3):
            c_a0(g, k).wait_send()
            c_a1(g, k).wait_send()
            c_a2(g, k).wait_send()
            c_a3(g, k).wait()
        return 0

    lax.fori_loop(0, NG, drain, 0)


def backward(x, dy, gate, up, w_gate, w_up, w_down, *, cb=512):
    rows, wide = x.shape
    ff = gate.shape[1]
    gr, half = rows // NG, wide // 2
    any_space = pl.BlockSpec(memory_space=pl.ANY)
    dma = pltpu.SemaphoreType.DMA
    return pl.pallas_call(
        functools.partial(kernel, cb=cb),
        out_shape=(
            jax.ShapeDtypeStruct((rows, wide), BF),
            jax.ShapeDtypeStruct((wide, ff), BF),
            jax.ShapeDtypeStruct((wide, ff), BF),
            jax.ShapeDtypeStruct((ff, wide), BF),
        ),
        in_specs=[any_space] * 7,
        out_specs=(any_space,) * 4,
        scratch_shapes=[
            pltpu.VMEM((rows, 2 * ff), BF),
            pltpu.VMEM((ff, rows), BF),
            pltpu.VMEM((gr, half), F32),
            pltpu.VMEM((gr // 2, half), F32),
            pltpu.VMEM((gr // 4, half), F32),
            pltpu.VMEM((gr // 8, half), F32),
            pltpu.VMEM((gr, half), BF),
            pltpu.VMEM((gr, half), BF),
            pltpu.VMEM((gr // 2, half), BF),
            pltpu.VMEM((gr // 4, half), BF),
            pltpu.VMEM((gr // 8, half), BF),
            pltpu.VMEM((NG, gr // 2, half), BF),
            pltpu.VMEM((NG, gr // 4, half), BF),
            pltpu.VMEM((NG, gr // 8, half), BF),
            pltpu.VMEM((NG, gr // 8, half), BF),
            dma((6,)),
            dma(()),
            dma(()),
            dma((3,)),
            dma((3,)),
            dma((3,)),
            *[dma((3, NG))] * 3,
            dma((3, NG)),
            *[dma((3, NG))] * 8,
            pltpu.SemaphoreType.REGULAR,
            dma((2, 3)),
        ],
        compiler_params=pltpu.CompilerParams(
            collective_id=0, has_side_effects=True, vmem_limit_bytes=67_043_328
        ),
        name="mlp_backward",
    )(x, dy, gate, up, w_gate, w_up, w_down)


def solution(mesh):
    tokens, columns, rows = P("dp", None), P(None, "tp"), P("tp", None)
    return jax.shard_map(
        backward,
        mesh=mesh,
        in_specs=(tokens, tokens, P("dp", "tp"), P("dp", "tp"), columns, columns, rows),
        out_specs=(tokens, P("dp", "tp"), P("dp", "tp"), P(("dp", "tp"), None)),
        check_vma=False,
    )
```

profile of v0, /device:TPU:0, one launch (start us, length us, event | category | flops | bytes accessed | tf_op | source)
XLA Modules:
  0.0 222.0 jit_solution(8629451428198973321)
XLA Ops:
  0.6 186.6 %mlp_backward.1 = (bf16[2048,5120]{1,0:T(8,128)(2,1)}, bf16[5120,768]{1,0:T(8,128)(2,1)}, bf16[5120,768]{1,0:T(8,128)(2,1)}, bf16[768,5120]{1,0:T(8,128)(2,1)}) custom-call(bf16[2048,5120]{1,0:T(8,128)(2,1)} %x.1, bf16[2048,5120]{1,0:T(8,128)(2,1)} %dy.1, bf16[2048,768]{1,0:T(8,128)(2,1)} %gate.1, bf16[2048,768]{1,0:T(8,128)(2,1)} %up.1, ...), custom_call_target="tpu_custom_call" | custom-call | tf_op jit(solution)/shard_map/mlp_backward/pallas_call | solution.py:352
  187.2 17.3 %copy.15 = bf16[2048,5120]{1,0:T(8,128)(2,1)} copy(bf16[2048,5120]{1,0:T(8,128)(2,1)} %get-tuple-element.8) | data formatting | bytes 41943040
  204.5 0.0 slice-start
  204.5 7.1 %copy.16 = bf16[5120,768]{1,0:T(8,128)(2,1)} copy(bf16[5120,768]{1,0:T(8,128)(2,1)} %get-tuple-element.9) | data formatting | bytes 15728640
  211.6 0.0 slice-start.1
  211.6 7.1 %copy.17 = bf16[5120,768]{1,0:T(8,128)(2,1)} copy(bf16[5120,768]{1,0:T(8,128)(2,1)} %get-tuple-element.10) | data formatting | bytes 15728640
  218.7 0.0 slice-done
  218.7 0.0 slice-done.1
  218.7 3.2 %copy.18 = bf16[768,5120]{1,0:T(8,128)(2,1)} copy(bf16[768,5120]{1,0:T(8,128)(2,1)S(1)} %bitcast.1) | data formatting | bytes 15728640
  (1 shorter events, 0.0 us)
Async XLA Ops:
  204.5 14.2 %slice-start = ((s8[7864320]{0:T(1024)(128)(4,1)}), s8[4194304]{0:T(1024)(128)(4,1)S(1)}, s32[]{:S(2)}) async-start(s8[7864320]{0:T(1024)(128)(4,1)} %bitcast), calls=%async_computation | async-start | bytes 8388608
  211.6 7.1 %slice-start.1 = ((s8[7864320]{0:T(1024)(128)(4,1)}), s8[3670016]{0:T(1024)(128)(4,1)S(1)}, s32[]{:S(2)}) async-start(s8[7864320]{0:T(1024)(128)(4,1)} %bitcast), calls=%async_computation.1 | async-start | bytes 7340032
where the time goes:
time: 222 us
  Pallas kernels  187 us (84%)
  local copies, waits for them, and re-layouts  34.7 us (16%)
    pallas_call x1, Pallas kernels, backward(): pl.pallas_call(functools.partial(kernel, cb=cb), out_shape=(jax.ShapeDtyp...  187 us
    unnamed x8, local copies, waits for them, and re-layouts  34.7 us

commit v1 on v0

--- a/solution.py
+++ b/solution.py
@@ -30,7 +30,7 @@
     x, dy, gate, up, w_gate, w_up, w_down,
     dx, dw_gate, dw_up, dw_down,
     d_all, hid_t, acc0, acc1, acc2, acc3, d2d_out, d2d_in, out1, out2, out3, in1, in2, in3, fin,
-    load, d2d_s, d2d_r, s1, s2, s3, r1, r2, r3, a_loc, a3s, a3r, a2s, a2r, a1s, a1r, ds, dr, credit, st,
+    load, d2d_s, d2d_r, s1, s2, s3, r1, r2, r3, a_loc, a3s, a3r, a2s, a2r, a1s, a1r, ds, dr, credit,
     *, cb,
 ):
     rows, wide = x.shape
@@ -44,8 +44,12 @@
     mine = pl.multiple_of(core * half, 128)
     other = pl.multiple_of((1 - core) * half, 128)
 
+    def stride_of(k, stage):
+        first, second = ORDERS[k][stage], ORDERS[(k + 1) % 3][stage]
+        return first + core * (second - first)
+
     def bit(stride):
-        return lax.rem(me // stride, 2)
+        return lax.rem(lax.div(me, stride), 2)
 
     def peer(stride):
         return me + (1 - 2 * bit(stride)) * stride
@@ -65,26 +69,26 @@
     def c_rs(stage, g, k):
         src, dst, send, recv = ((out1, in1, s1, r1), (out2, in2, s2, r2), (out3, in3, s3, r3))[stage]
         c = pl.ds(*cols[k])
-        return remote(src.at[:, c], dst.at[g, :, c], send.at[k], recv.at[k, g], peer(ORDERS[k][stage]))
+        return remote(src.at[:, c], dst.at[g, :, c], send.at[k], recv.at[k, g], peer(stride_of(k, stage)))
 
     def region(g, k, depth):
         start, size = g * g_rows, g_rows
         for stage in range(depth):
             size //= 2
-            start = start + bit(ORDERS[k][stage]) * size
+            start = start + bit(stride_of(k, stage)) * size
         return dx.at[rows_at(start, size), pl.ds(pl.multiple_of(mine + cols[k][0], 128), cols[k][1])]
 
     def c_local(g, k):
         return pltpu.make_async_copy(fin.at[g, :, pl.ds(*cols[k])], region(g, k, 3), a_loc.at[k, g])
 
     def c_a0(g, k):
-        return remote(fin.at[g, :, pl.ds(*cols[k])], region(g, k, 3), a3s.at[k, g], a3r.at[k, g], peer(ORDERS[k][2]))
+        return remote(fin.at[g, :, pl.ds(*cols[k])], region(g, k, 3), a3s.at[k, g], a3r.at[k, g], peer(stride_of(k, 2)))
 
     def c_a1(g, k):
-        return remote(region(g, k, 2), region(g, k, 2), a2s.at[k, g], a2r.at[k, g], peer(ORDERS[k][1]))
+        return remote(region(g, k, 2), region(g, k, 2), a2s.at[k, g], a2r.at[k, g], peer(stride_of(k, 1)))
 
     def c_a2(g, k):
-        return remote(region(g, k, 1), region(g, k, 1), a1s.at[k, g], a1r.at[k, g], peer(ORDERS[k][0]))
+        return remote(region(g, k, 1), region(g, k, 1), a1s.at[k, g], a1r.at[k, g], peer(stride_of(k, 0)))
 
     def c_a3(g, k):
         return remote(region(g, k, 0), region(g, k, 0), ds.at[k, g], dr.at[k, g], sib)
@@ -94,7 +98,7 @@
         h = g_rows // 2
         for k in range(3):
             c = pl.ds(*cols[k])
-            away = rows_at((1 - bit(ORDERS[k][0])) * h, h)
+            away = rows_at((1 - bit(stride_of(k, 0))) * h, h)
 
             @pl.when(g > 0)
             def _():
@@ -104,7 +108,7 @@
             c_rs(0, g, k).start()
         for k in range(3):
             c = pl.ds(*cols[k])
-            keep = rows_at(bit(ORDERS[k][0]) * h, h)
+            keep = rows_at(bit(stride_of(k, 0)) * h, h)
             acc1[:, c] = acc0[keep, c] + d2d_in[keep, c].astype(F32)
 
         @pl.when(g < NG - 1)
@@ -116,7 +120,7 @@
         for k in range(3):
             c = pl.ds(*cols[k])
             c_rs(stage - 1, g, k).wait_recv()
-            away = rows_at((1 - bit(ORDERS[k][stage])) * h, h)
+            away = rows_at((1 - bit(stride_of(k, stage))) * h, h)
 
             @pl.when(g > 0)
             def _():
@@ -124,7 +128,7 @@
 
             out[:, c] = (src[away, c] + came[g, away, c].astype(F32)).astype(BF)
             c_rs(stage, g, k).start()
-            keep = rows_at(bit(ORDERS[k][stage]) * h, h)
+            keep = rows_at(bit(stride_of(k, stage)) * h, h)
             dst[:, c] = src[keep, c] + came[g, keep, c].astype(F32)
 
     def e4(g):
@@ -170,19 +174,21 @@
             reduce_events(NG + s)
             at(s >= 0, a0, NG + s - 3)
 
-        for lag, f in ((5, a3), (3, a2), (1, a1)):
-            t = s - lag
-            g = lax.div(2 * jnp.maximum(t, 0), 5)
-            at((t >= 0) & (lax.rem(2 * jnp.maximum(t, 0), 5) < 2) & (g < NG), f, g)
-
-    last_slot = 5 + (5 * (NG - 1) + 1) // 2
+        for first, num, den, f in ((6, 2, 1, a3), (3, 8, 5, a2), (1, 1, 1, a1)):
+            t = den * jnp.maximum(s - first, 0)
+            g = lax.div(t, num)
+            at((s >= first) & (lax.rem(t, num) < den) & (g < NG), f, g)
+
+    last_slot = 6 + 2 * (NG - 1)
 
     barrier = pltpu.get_barrier_semaphore()
     for to in (sib, peer(8), peer(4), peer(2)):
         pl.semaphore_signal(barrier, inc=1, device_id={"tp": to}, device_id_type=MESH)
     pl.semaphore_wait(barrier, 4)
 
-    def first_phase(wd, wg, wu, dyb, gb, ub):
+    wd, wg, wu = dw_down, dw_gate, dw_up
+
+    def first_phase(dyb, gb, ub):
         def rows_of(g):
             r = rows_at(g * g_rows, g_rows)
             return (
@@ -247,15 +253,12 @@
 
     pl.run_scoped(
         first_phase,
-        pltpu.VMEM((ff, wide), BF),
-        pltpu.VMEM((wide, ff), BF),
-        pltpu.VMEM((wide, ff), BF),
         pltpu.VMEM((g_rows, wide), BF),
         pltpu.VMEM((g_rows, ff), BF),
         pltpu.VMEM((g_rows, ff), BF),
     )
 
-    def second_phase(xb, yb, og, od):
+    def second_phase(xb, yb):
         def loads(i, b):
             c = rows_at(i * cb, cb)
             return (
@@ -263,14 +266,6 @@
                 pltpu.make_async_copy(dy.at[:, c], yb.at[b], load.at[2 + b]),
             )
 
-        def stores(i, b):
-            c = rows_at(i * cb, cb)
-            return (
-                pltpu.make_async_copy(og.at[b, :, pl.ds(0, ff)], dw_gate.at[c], st.at[b, 0]),
-                pltpu.make_async_copy(og.at[b, :, pl.ds(ff, ff)], dw_up.at[c], st.at[b, 1]),
-                pltpu.make_async_copy(od.at[b], dw_down.at[:, c], st.at[b, 2]),
-            )
-
         for c in loads(0, 0):
             c.start()
 
@@ -289,36 +284,23 @@
                     c.start()
 
             into = loads(i, b)
-            out = stores(i, b)
-
-            @pl.when(i >= 2)
-            def _():
-                for c in out:
-                    c.wait()
-
+            c = rows_at(i * cb, cb)
             into[0].wait()
-            og[b] = dot(xb[b], d_all[...], TN).astype(BF)
-            out[0].start()
-            out[1].start()
+            both = dot(xb[b], d_all[...], TN).astype(BF)
+            dw_gate[c, :] = both[:, :ff]
+            dw_up[c, :] = both[:, ff:]
             slot(2 * i)
             into[1].wait()
-            od[b] = dot(hid_t[...], yb[b], NN).astype(BF)
-            out[2].start()
+            dw_down[:, c] = dot(hid_t[...], yb[b], NN).astype(BF)
             slot(2 * i + 1)
             return 0
 
         lax.fori_loop(0, steps, body, 0)
-
-        for i in (steps - 2, steps - 1):
-            for c in stores(i, i % 2):
-                c.wait()
 
     pl.run_scoped(
         second_phase,
         pltpu.VMEM((2, rows, cb), BF),
         pltpu.VMEM((2, rows, cb), BF),
-        pltpu.VMEM((2, cb, 2 * ff), BF),
-        pltpu.VMEM((2, ff, cb), BF),
     )
 
     def rest(s, _):
@@ -349,16 +331,16 @@
     gr, half = rows // NG, wide // 2
     any_space = pl.BlockSpec(memory_space=pl.ANY)
     dma = pltpu.SemaphoreType.DMA
-    return pl.pallas_call(
+    grads = pl.pallas_call(
         functools.partial(kernel, cb=cb),
         out_shape=(
             jax.ShapeDtypeStruct((rows, wide), BF),
-            jax.ShapeDtypeStruct((wide, ff), BF),
-            jax.ShapeDtypeStruct((wide, ff), BF),
-            jax.ShapeDtypeStruct((ff, wide), BF),
+            pltpu.VMEM((wide, ff), BF),
+            pltpu.VMEM((wide, ff), BF),
+            pltpu.VMEM((ff, wide), BF),
         ),
         in_specs=[any_space] * 7,
-        out_specs=(any_space,) * 4,
+        out_specs=(any_space, *[pl.BlockSpec(memory_space=pltpu.VMEM)] * 3),
         scratch_shapes=[
             pltpu.VMEM((rows, 2 * ff), BF),
             pltpu.VMEM((ff, rows), BF),
@@ -385,13 +367,61 @@
             dma((3, NG)),
             *[dma((3, NG))] * 8,
             pltpu.SemaphoreType.REGULAR,
-            dma((2, 3)),
         ],
         compiler_params=pltpu.CompilerParams(
-            collective_id=0, has_side_effects=True, vmem_limit_bytes=67_043_328
+            collective_id=0, has_side_effects=True, vmem_limit_bytes=43_200_000
         ),
         name="mlp_backward",
     )(x, dy, gate, up, w_gate, w_up, w_down)
+    return write_out(*grads)
+
+
+def write_kernel(dx, a, b, c, dx_o, a_o, b_o, c_o, buf, rd, wr, sem):
+    slots, piece, _ = buf.shape
+    n = dx.shape[0] // piece
+
+    def read(i):
+        return pltpu.make_async_copy(dx.at[pl.ds(i * piece, piece)], buf.at[i % slots], rd.at[i % slots])
+
+    def write(i):
+        return pltpu.make_async_copy(buf.at[i % slots], dx_o.at[pl.ds(i * piece, piece)], wr.at[i % slots])
+
+    rest = [pltpu.make_async_copy(s, d, sem.at[i]) for i, (s, d) in enumerate(((a, a_o), (b, b_o), (c, c_o)))]
+    for i in range(min(slots, n)):
+        read(i).start()
+    for r in rest:
+        r.start()
+    for i in range(n):
+        read(i).wait()
+        write(i).start()
+        if i + slots < n:
+            write(i).wait()
+            read(i + slots).start()
+    for i in range(max(n - slots, 0), n):
+        write(i).wait()
+    for r in rest:
+        r.wait()
+
+
+def write_out(dx, a, b, c, *, pieces=16, slots=8):
+    any_space = pl.BlockSpec(memory_space=pl.ANY)
+    vmem = pl.BlockSpec(memory_space=pltpu.VMEM)
+    dma = pltpu.SemaphoreType.DMA
+    rows, wide = dx.shape
+    return pl.pallas_call(
+        write_kernel,
+        out_shape=tuple(jax.ShapeDtypeStruct(r.shape, BF) for r in (dx, a, b, c)),
+        in_specs=[any_space, vmem, vmem, vmem],
+        out_specs=(any_space,) * 4,
+        scratch_shapes=[
+            pltpu.VMEM((slots, rows // pieces, wide), BF),
+            dma((slots,)),
+            dma((slots,)),
+            dma((3,)),
+        ],
+        compiler_params=pltpu.CompilerParams(vmem_limit_bytes=12_000_000),
+        name="write_out",
+    )(dx, a, b, c)
 
 
 def solution(mesh):

time: 222 us -> 201 us (0.905)
  local copies, waits for them, and re-layouts: 34.7 us -> 0 us
  Pallas kernels: 187 us -> 200 us
    unnamed x8 -> x0, local copies, waits for them, and re-layouts: 34.7 us -> none
    pallas_call x0 -> x1, Pallas kernels: none -> 23 us  [write_out(): pl.pallas_call(write_kernel, out_shape=tuple((jax.ShapeDtypeStruct(r.shap...]
    pallas_call x1, Pallas kernels: 187 us -> 177 us  [backward(): pl.pallas_call(functools.partial(kernel, cb=cb), out_shape=(jax.ShapeDtyp...]
where the time goes in v1:
time: 201 us
  Pallas kernels  200 us (100%)
    pallas_call x1, Pallas kernels, backward(): pl.pallas_call(functools.partial(kernel, cb=cb), out_shape=(jax.ShapeDtyp...  177 us
    pallas_call x1, Pallas kernels, write_out(): pl.pallas_call(write_kernel, out_shape=tuple((jax.ShapeDtypeStruct(r.shap...  23 us

profile of v1, /device:TPU:0, one launch (start us, length us, event | category | flops | bytes accessed | tf_op | source)
XLA Modules:
  0.0 200.5 jit_solution(17643739427509281845)
XLA Ops:
  0.6 176.9 %mlp_backward.1 = (bf16[2048,5120]{1,0:T(8,128)(2,1)}, bf16[5120,768]{1,0:T(8,128)(2,1)S(1)}, bf16[5120,768]{1,0:T(8,128)(2,1)S(1)}, bf16[768,5120]{1,0:T(8,128)(2,1)S(1)}) custom-call(bf16[2048,5120]{1,0:T(8,128)(2,1)} %x.1, bf16[2048,5120]{1,0:T(8,128)(2,1)} %dy.1, bf16[2048,768]{1,0:T(8,128)(2,1)} %gate.1, bf16[2048,768]{1,0:T(8,128)(2,1)} %up.1, ...), custom_call_target="tpu_custom_call" | custom-call | tf_op jit(solution)/shard_map/mlp_backward/pallas_call | solution.py:334
  177.5 23.0 %write_out.1 = (bf16[2048,5120]{1,0:T(8,128)(2,1)}, bf16[5120,768]{1,0:T(8,128)(2,1)}, bf16[5120,768]{1,0:T(8,128)(2,1)}, bf16[768,5120]{1,0:T(8,128)(2,1)}) custom-call(bf16[2048,5120]{1,0:T(8,128)(2,1)} %get-tuple-element.8.dx, bf16[5120,768]{1,0:T(8,128)(2,1)S(1)} %get-tuple-element.9.a, bf16[5120,768]{1,0:T(8,128)(2,1)S(1)} %get-tuple-element.10.b, ...), custom_call_target="tpu_custom_call" | custom-call | tf_op jit(solution)/shard_map/write_out/pallas_call | solution.py:411

commit v2 on v1

--- a/solution.py
+++ b/solution.py
@@ -28,7 +28,7 @@
 
 def kernel(
     x, dy, gate, up, w_gate, w_up, w_down,
-    dx, dw_gate, dw_up, dw_down,
+    dx, dw_in, dw_down,
     d_all, hid_t, acc0, acc1, acc2, acc3, d2d_out, d2d_in, out1, out2, out3, in1, in2, in3, fin,
     load, d2d_s, d2d_r, s1, s2, s3, r1, r2, r3, a_loc, a3s, a3r, a2s, a2r, a1s, a1r, ds, dr, credit,
     *, cb,
@@ -184,9 +184,8 @@
     barrier = pltpu.get_barrier_semaphore()
     for to in (sib, peer(8), peer(4), peer(2)):
         pl.semaphore_signal(barrier, inc=1, device_id={"tp": to}, device_id_type=MESH)
-    pl.semaphore_wait(barrier, 4)
-
-    wd, wg, wu = dw_down, dw_gate, dw_up
+
+    wd, w_in = dw_down, dw_in
 
     def first_phase(dyb, gb, ub):
         def rows_of(g):
@@ -197,13 +196,19 @@
                 pltpu.make_async_copy(up.at[r], ub, load.at[2]),
             )
 
-        weights = [pltpu.make_async_copy(a, b, load.at[3 + i]) for i, (a, b) in enumerate(((w_down, wd), (w_gate, wg), (w_up, wu)))]
-        weights[0].start()
-        for c in rows_of(0):
+        def w_half(start, i):
+            r = pl.ds(start, half)
+            return [
+                pltpu.make_async_copy(w.at[r], w_in.at[r, pl.ds(j * ff, ff)], load.at[4 + 2 * i + j])
+                for j, w in enumerate((w_gate, w_up))
+            ]
+
+        w_first = pltpu.make_async_copy(w_down, wd, load.at[3])
+        w_other, w_mine = w_half(other, 0), w_half(mine, 1)
+        for c in (w_first, *rows_of(0), *w_other, *w_mine):
             c.start()
-        weights[1].start()
-        weights[2].start()
-        weights[0].wait()
+        pl.semaphore_wait(barrier, 4)
+        w_first.wait()
 
         def body(g, _):
             for c in rows_of(g):
@@ -222,16 +227,16 @@
                 for c in rows_of(jnp.minimum(g + 1, NG - 1)):
                     c.start()
 
-            @pl.when(g == 0)
-            def _():
-                weights[1].wait()
-                weights[2].wait()
-
-            dg, du = d_all[r, pl.ds(0, ff)], d_all[r, pl.ds(ff, ff)]
+            def when_first(copies):
+                @pl.when(g == 0)
+                def _():
+                    for c in copies:
+                        c.wait()
 
             def term(start):
-                w = pl.ds(start, half)
-                return dot(dg, wg[w, :], NT) + dot(du, wu[w, :], NT)
+                return dot(d_all[r, :], w_in[pl.ds(start, half), :], NT)
+
+            when_first(w_other)
 
             @pl.when(g > 0)
             def _():
@@ -244,6 +249,7 @@
                 pl.semaphore_wait(credit, 1)
 
             c_d2d().start()
+            when_first(w_mine)
             acc0[...] = term(mine)
             reduce_events(g)
             e1(g)
@@ -286,9 +292,7 @@
             into = loads(i, b)
             c = rows_at(i * cb, cb)
             into[0].wait()
-            both = dot(xb[b], d_all[...], TN).astype(BF)
-            dw_gate[c, :] = both[:, :ff]
-            dw_up[c, :] = both[:, ff:]
+            dw_in[c, :] = dot(xb[b], d_all[...], TN).astype(BF)
             slot(2 * i)
             into[1].wait()
             dw_down[:, c] = dot(hid_t[...], yb[b], NN).astype(BF)
@@ -335,12 +339,11 @@
         functools.partial(kernel, cb=cb),
         out_shape=(
             jax.ShapeDtypeStruct((rows, wide), BF),
-            pltpu.VMEM((wide, ff), BF),
-            pltpu.VMEM((wide, ff), BF),
+            pltpu.VMEM((wide, 2 * ff), BF),
             pltpu.VMEM((ff, wide), BF),
         ),
         in_specs=[any_space] * 7,
-        out_specs=(any_space, *[pl.BlockSpec(memory_space=pltpu.VMEM)] * 3),
+        out_specs=(any_space, *[pl.BlockSpec(memory_space=pltpu.VMEM)] * 2),
         scratch_shapes=[
             pltpu.VMEM((rows, 2 * ff), BF),
             pltpu.VMEM((ff, rows), BF),
@@ -357,7 +360,7 @@
             pltpu.VMEM((NG, gr // 4, half), BF),
             pltpu.VMEM((NG, gr // 8, half), BF),
             pltpu.VMEM((NG, gr // 8, half), BF),
-            dma((6,)),
+            dma((8,)),
             dma(()),
             dma(()),
             dma((3,)),
@@ -376,7 +379,7 @@
     return write_out(*grads)
 
 
-def write_kernel(dx, a, b, c, dx_o, a_o, b_o, c_o, buf, rd, wr, sem):
+def write_kernel(dx, ab, c, dx_o, a_o, b_o, c_o, buf, rd, wr, sem):
     slots, piece, _ = buf.shape
     n = dx.shape[0] // piece
 
@@ -386,7 +389,9 @@
     def write(i):
         return pltpu.make_async_copy(buf.at[i % slots], dx_o.at[pl.ds(i * piece, piece)], wr.at[i % slots])
 
-    rest = [pltpu.make_async_copy(s, d, sem.at[i]) for i, (s, d) in enumerate(((a, a_o), (b, b_o), (c, c_o)))]
+    ff = a_o.shape[1]
+    parts = ((ab.at[:, pl.ds(0, ff)], a_o), (ab.at[:, pl.ds(ff, ff)], b_o), (c, c_o))
+    rest = [pltpu.make_async_copy(s, d, sem.at[i]) for i, (s, d) in enumerate(parts)]
     for i in range(min(slots, n)):
         read(i).start()
     for r in rest:
@@ -403,15 +408,16 @@
         r.wait()
 
 
-def write_out(dx, a, b, c, *, pieces=16, slots=8):
+def write_out(dx, ab, c, *, pieces=16, slots=8):
     any_space = pl.BlockSpec(memory_space=pl.ANY)
     vmem = pl.BlockSpec(memory_space=pltpu.VMEM)
     dma = pltpu.SemaphoreType.DMA
     rows, wide = dx.shape
+    ff = c.shape[0]
     return pl.pallas_call(
         write_kernel,
-        out_shape=tuple(jax.ShapeDtypeStruct(r.shape, BF) for r in (dx, a, b, c)),
-        in_specs=[any_space, vmem, vmem, vmem],
+        out_shape=tuple(jax.ShapeDtypeStruct(r, BF) for r in (dx.shape, (wide, ff), (wide, ff), c.shape)),
+        in_specs=[any_space, vmem, vmem],
         out_specs=(any_space,) * 4,
         scratch_shapes=[
             pltpu.VMEM((slots, rows // pieces, wide), BF),
@@ -421,7 +427,7 @@
         ],
         compiler_params=pltpu.CompilerParams(vmem_limit_bytes=12_000_000),
         name="write_out",
-    )(dx, a, b, c)
+    )(dx, ab, c)
 
 
 def solution(mesh):

time: 201 us -> 194 us (0.965)
  Pallas kernels: 200 us -> 193 us
    pallas_call x1, Pallas kernels: 177 us -> 170 us  [backward(): pl.pallas_call(functools.partial(kernel, cb=cb), out_shape=(jax.ShapeDtyp...]
where the time goes in v2:
time: 194 us
  Pallas kernels  193 us (99%)
    pallas_call x1, Pallas kernels, backward(): pl.pallas_call(functools.partial(kernel, cb=cb), out_shape=(jax.ShapeDtyp...  170 us
    pallas_call x1, Pallas kernels, write_out(): pl.pallas_call(write_kernel, out_shape=tuple((jax.ShapeDtypeStruct(r, BF)...  23 us

profile of v2, /device:TPU:0, one launch (start us, length us, event | category | flops | bytes accessed | tf_op | source)
XLA Modules:
  0.0 193.6 jit_solution(4498701304146621302)
XLA Ops:
  0.6 170.0 %mlp_backward.1 = (bf16[2048,5120]{1,0:T(8,128)(2,1)}, bf16[5120,1536]{1,0:T(8,128)(2,1)S(1)}, bf16[768,5120]{1,0:T(8,128)(2,1)S(1)}) custom-call(bf16[2048,5120]{1,0:T(8,128)(2,1)} %x.1, bf16[2048,5120]{1,0:T(8,128)(2,1)} %dy.1, bf16[2048,768]{1,0:T(8,128)(2,1)} %gate.1, bf16[2048,768]{1,0:T(8,128)(2,1)} %up.1, bf16[5120,768]{1,0:T(8,128)(2,1)} %w_gate.1, ...), custom_call_target="tpu_custom_call" | custom-call | tf_op jit(solution)/shard_map/mlp_backward/pallas_call | solution.py:338
  170.6 23.0 %write_out.1 = (bf16[2048,5120]{1,0:T(8,128)(2,1)}, bf16[5120,768]{1,0:T(8,128)(2,1)}, bf16[5120,768]{1,0:T(8,128)(2,1)}, bf16[768,5120]{1,0:T(8,128)(2,1)}) custom-call(bf16[2048,5120]{1,0:T(8,128)(2,1)} %get-tuple-element.7.dx, bf16[5120,1536]{1,0:T(8,128)(2,1)S(1)} %get-tuple-element.8.ab, bf16[768,5120]{1,0:T(8,128)(2,1)S(1)} %get-tuple-element.9.c), custom_call_target="tpu_custom_call" | custom-call | tf_op jit(solution)/shard_map/write_out/pallas_call | solution.py:417

commit v3 on v2

v3 whole, which is shorter than its diff:
```python
import functools

import jax
import jax.numpy as jnp
from jax import lax
from jax.experimental import pallas as pl
from jax.experimental.pallas import tpu as pltpu
from jax.sharding import PartitionSpec as P

MESH = pl.DeviceIdType.MESH
BF, F32 = jnp.bfloat16, jnp.float32
NT = (((1,), (1,)), ((), ()))
TN = (((0,), (0,)), ((), ()))
NN = (((1,), (0,)), ((), ()))
NG = 8
ORDERS = ((8, 4, 2), (4, 2, 8), (2, 8, 4))


def dot(a, b, dims):
    return lax.dot_general(a, b, dims, preferred_element_type=F32)


def colours(half):
    tiles = half // 128
    widths = [128 * ((tiles + 2 - k) // 3) for k in range(3)]
    return [(sum(widths[:k]), widths[k]) for k in range(3)]


def kernel(
    x, dy, gate, up, w_gate, w_up, w_down,
    dx, dw_gate, dw_up, dw_down, d_kept, hid_kept,
    acc1, acc2, acc3, d2d_out, out1, out2, out3,
    load, d2d_s, d2d_r, s1, s2, s3, r1, r2, r3, a3s, a3r, a2s, a2r, a1s, a1r, ds, dr, credit,
    *, cb,
):
    rows, wide = x.shape
    ff = gate.shape[1]
    g_rows, half = rows // NG, wide // 2
    cols = colours(half)
    steps = wide // cb
    me = lax.axis_index("tp")
    core = lax.rem(me, 2)
    sib = me + 1 - 2 * core
    mine = pl.multiple_of(core * half, 128)
    other = pl.multiple_of((1 - core) * half, 128)

    def stride_of(k, stage):
        first, second = ORDERS[k][stage], ORDERS[(k + 1) % 3][stage]
        return first + core * (second - first)

    def bit(stride):
        return lax.rem(lax.div(me, stride), 2)

    def peer(stride):
        return me + (1 - 2 * bit(stride)) * stride

    def rows_at(start, size):
        return pl.ds(pl.multiple_of(start, size), size)

    def remote(src, dst, send, recv, to):
        return pltpu.make_async_remote_copy(
            src_ref=src, dst_ref=dst, send_sem=send, recv_sem=recv,
            device_id={"tp": to}, device_id_type=MESH,
        )

    def own(g, k, start, size):
        return rows_at(start + g * g_rows, size), pl.ds(pl.multiple_of(mine + cols[k][0], 128), cols[k][1])

    def landing(g, k, stage, b):
        h = g_rows // 2
        start, size = ((b * h, h), ((1 - b) * h, h // 2), ((1 - b) * h + h // 2, h // 4))[stage]
        return start, size

    def came(g, k, stage, start, size):
        first, _ = landing(g, k, stage, bit(stride_of(k, 0)))
        return dx[own(g, k, first + start, size)].astype(F32)

    def c_d2d(g):
        return remote(d2d_out, dx.at[rows_at(g * g_rows, g_rows), pl.ds(mine, half)], d2d_s, d2d_r.at[g], sib)

    def c_rs(stage, g, k):
        src, send, recv = ((out1, s1, r1), (out2, s2, r2), (out3, s3, r3))[stage]
        b = bit(stride_of(k, 0))
        dst = own(g, k, *landing(g, k, stage, 1 - b if stage == 0 else b))
        return remote(src.at[:, pl.ds(*cols[k])], dx.at[dst], send.at[k], recv.at[k, g], peer(stride_of(k, stage)))

    def held(k, depth):
        start, size = 0, g_rows
        for stage in range(depth):
            size //= 2
            start = start + bit(stride_of(k, stage)) * size
        return start, size

    def region(g, k, depth):
        return dx.at[own(g, k, *held(k, depth))]

    def c_a0(g, k):
        return remote(region(g, k, 3), region(g, k, 3), a3s.at[k, g], a3r.at[k, g], peer(stride_of(k, 2)))

    def c_a1(g, k):
        return remote(region(g, k, 2), region(g, k, 2), a2s.at[k, g], a2r.at[k, g], peer(stride_of(k, 1)))

    def c_a2(g, k):
        return remote(region(g, k, 1), region(g, k, 1), a1s.at[k, g], a1r.at[k, g], peer(stride_of(k, 0)))

    def c_a3(g, k):
        return remote(region(g, k, 0), region(g, k, 0), ds.at[k, g], dr.at[k, g], sib)

    def e1(g, acc0):
        c_d2d(g).wait_recv()
        h = g_rows // 2

        def chip_sum(k, start):
            theirs = dx[rows_at(g * g_rows + start, h), pl.ds(pl.multiple_of(other + cols[k][0], 128), cols[k][1])]
            return acc0[rows_at(start, h), pl.ds(*cols[k])] + theirs.astype(F32)

        for k in range(3):

            @pl.when(g > 0)
            def _():
                c_rs(0, g, k).wait_send()

            out1[:, pl.ds(*cols[k])] = chip_sum(k, (1 - bit(stride_of(k, 0))) * h).astype(BF)
            c_rs(0, g, k).start()
        for k in range(3):
            acc1[:, pl.ds(*cols[k])] = chip_sum(k, bit(stride_of(k, 0)) * h)

    def e_mid(stage, g, src, out, dst):
        h = src.shape[0] // 2
        for k in range(3):
            c = pl.ds(*cols[k])
            c_rs(stage - 1, g, k).wait_recv()
            away = (1 - bit(stride_of(k, stage))) * h
            keep = bit(stride_of(k, stage)) * h

            @pl.when(g > 0)
            def _():
                c_rs(stage, g, k).wait_send()

            out[:, c] = (src[rows_at(away, h), c] + came(g, k, stage - 1, away, h)).astype(BF)
            c_rs(stage, g, k).start()
            dst[:, c] = src[rows_at(keep, h), c] + came(g, k, stage - 1, keep, h)

    def e4(g):
        for k in range(3):
            c_rs(2, g, k).wait_recv()
            size = acc3.shape[0]
            total = acc3[:, pl.ds(*cols[k])] + came(g, k, 2, 0, size)
            dx[own(g, k, *held(k, 3))] = total.astype(BF)

    def a0(g):
        for k in range(3):
            c_a0(g, k).start()

    def at(cond, f, g):
        @pl.when(cond)
        def _():
            f(g)

    def reduce_events(t):
        at((t >= 3) & (t < NG + 3), e4, t - 3)
        at((t >= 2) & (t < NG + 2), lambda g: e_mid(2, g, acc2, out3, acc3), t - 2)
        at((t >= 1) & (t < NG + 1), lambda g: e_mid(1, g, acc1, out2, acc2), t - 1)

    def a1(g):
        for k in range(3):
            c_a0(g, k).wait_recv()
            c_a1(g, k).start()

    def a2(g):
        for k in range(3):
            c_a1(g, k).wait_recv()
            c_a2(g, k).start()

    def a3(g):
        for k in range(3):
            c_a2(g, k).wait_recv()
            c_a3(g, k).start()

    def slot(s):
        @pl.when(s < 3)
        def _():
            reduce_events(NG + s)
            at(s >= 0, a0, NG + s - 3)

        @pl.when(s == 2)
        def _():
            for to in (sib, peer(8), peer(4), peer(2)):
                pl.semaphore_signal(credit, inc=1, device_id={"tp": to}, device_id_type=MESH)

        @pl.when(s == 3)
        def _():
            pl.semaphore_wait(credit, 4)

        for first, num, den, f in ((6, 2, 1, a3), (3, 8, 5, a2), (1, 1, 1, a1)):
            t = den * jnp.maximum(s - first, 0)
            g = lax.div(t, num)
            at((s >= first) & (lax.rem(t, num) < den) & (g < NG), f, g)

    last_slot = 6 + 2 * (NG - 1)

    barrier = pltpu.get_barrier_semaphore()
    for to in (sib, peer(8), peer(4), peer(2)):
        pl.semaphore_signal(barrier, inc=1, device_id={"tp": to}, device_id_type=MESH)

    wd, wg, wu = dw_down, dw_gate, dw_up

    def first_phase(acc0, dyb, gb, ub, d_in, hid):
        def rows_of(g):
            r = rows_at(g * g_rows, g_rows)
            return (
                pltpu.make_async_copy(dy.at[r], dyb, load.at[0]),
                pltpu.make_async_copy(gate.at[r], gb, load.at[1]),
                pltpu.make_async_copy(up.at[r], ub, load.at[2]),
            )

        def keep(g):
            r = rows_at(g * g_rows, g_rows)
            return (
                pltpu.make_async_copy(d_in, d_kept.at[r], load.at[8]),
                pltpu.make_async_copy(hid, hid_kept.at[:, r], load.at[9]),
            )

        def w_half(start, i):
            r = pl.ds(start, half)
            return [
                pltpu.make_async_copy(w.at[r], v.at[r], load.at[4 + 2 * i + j])
                for j, (w, v) in enumerate(((w_gate, wg), (w_up, wu)))
            ]

        w_first = pltpu.make_async_copy(w_down, wd, load.at[3])
        w_other, w_mine = w_half(other, 0), w_half(mine, 1)
        for c in (w_first, *rows_of(0), *w_other, *w_mine):
            c.start()
        pl.semaphore_wait(barrier, 4)
        w_first.wait()

        def body(g, _):
            for c in rows_of(g):
                c.wait()
            @pl.when(g < NG)
            def _():
                acc0[:, pl.ds(0, ff)] = dot(dyb[...], wd[...], NT)

            d_h = acc0[:, pl.ds(0, ff)]
            gf, uf = gb[...].astype(F32), ub[...].astype(F32)
            sig = jax.nn.sigmoid(gf)
            silu = gf * sig

            @pl.when(g > 0)
            def _():
                for c in keep(g):
                    c.wait()

            d_in[:, pl.ds(0, ff)] = (d_h * uf * (sig + silu * (1 - sig))).astype(BF)
            d_in[:, pl.ds(ff, ff)] = (d_h * silu).astype(BF)
            hid[...] = (silu * uf).astype(BF).T
            for c in keep(g):
                c.start()

            @pl.when(g < NG - 1)
            def _():
                for c in rows_of(jnp.minimum(g + 1, NG - 1)):
                    c.start()

            def when_first(copies):
                @pl.when(g == 0)
                def _():
                    for c in copies:
                        c.wait()

            def term(start):
                w = pl.ds(start, half)
                return dot(d_in[:, pl.ds(0, ff)], wg[w, :], NT) + dot(d_in[:, pl.ds(ff, ff)], wu[w, :], NT)

            when_first(w_other)

            @pl.when(g > 0)
            def _():
                c_d2d(g).wait_send()

            @pl.when(g < NG)
            def _():
                acc0[...] = term(other)

            d2d_out[...] = acc0[...].astype(BF)

            c_d2d(g).start()
            when_first(w_mine)
            @pl.when(g < NG)
            def _():
                acc0[...] = term(mine)

            reduce_events(g)
            e1(g, acc0)
            return 0

        lax.fori_loop(0, NG, body, 0)
        for c in keep(NG - 1):
            c.wait()

    pl.run_scoped(
        first_phase,
        pltpu.VMEM((g_rows, half), F32),
        pltpu.VMEM((g_rows, wide), BF),
        pltpu.VMEM((g_rows, ff), BF),
        pltpu.VMEM((g_rows, ff), BF),
        pltpu.VMEM((g_rows, 2 * ff), BF),
        pltpu.VMEM((ff, g_rows), BF),
    )

    def second_phase(d_all, hid_t, xb, yb):
        again = (pltpu.make_async_copy(d_kept, d_all, load.at[8]), pltpu.make_async_copy(hid_kept, hid_t, load.at[9]))
        for c in again:
            c.start()

        def loads(i, b):
            c = rows_at(i * cb, cb)
            return (
                pltpu.make_async_copy(x.at[:, c], xb.at[b], load.at[b]),
                pltpu.make_async_copy(dy.at[:, c], yb.at[b], load.at[2 + b]),
            )

        for c in loads(0, 0):
            c.start()

        def early(g, _):
            a0(g)
            return 0

        lax.fori_loop(0, NG - 3, early, 0)
        for c in again:
            c.wait()

        def body(i, _):
            b = lax.rem(i, 2)

            @pl.when(i < steps - 1)
            def _():
                for c in loads(jnp.minimum(i + 1, steps - 1), 1 - b):
                    c.start()

            into = loads(i, b)
            c = rows_at(i * cb, cb)
            into[0].wait()

            @pl.when(i < steps)
            def _():
                both = dot(xb[b], d_all[...], TN).astype(BF)
                dw_gate[c, :] = both[:, :ff]
                dw_up[c, :] = both[:, ff:]

            into[1].wait()

            @pl.when(i < steps)
            def _():
                dw_down[:, c] = dot(hid_t[...], yb[b], NN).astype(BF)

            slot(i)
            return 0

        lax.fori_loop(0, steps, body, 0)

    pl.run_scoped(
        second_phase,
        pltpu.VMEM((rows, 2 * ff), BF),
        pltpu.VMEM((ff, rows), BF),
        pltpu.VMEM((2, rows, cb), BF),
        pltpu.VMEM((2, rows, cb), BF),
    )

    def rest(s, _):
        slot(s)
        return 0

    lax.fori_loop(steps, last_slot + 1, rest, 0)

    for k in range(3):
        for stage in range(3):
            c_rs(stage, NG - 1, k).wait_send()
    c_d2d(NG - 1).wait_send()

    def drain(g, _):
        for k in range(3):
            c_a0(g, k).wait_send()
            c_a1(g, k).wait_send()
            c_a2(g, k).wait_send()
            c_a3(g, k).wait()
        return 0

    lax.fori_loop(0, NG, drain, 0)


def backward(x, dy, gate, up, w_gate, w_up, w_down, *, cb=256):
    rows, wide = x.shape
    ff = gate.shape[1]
    gr, half = rows // NG, wide // 2
    any_space = pl.BlockSpec(memory_space=pl.ANY)
    dma = pltpu.SemaphoreType.DMA
    grads = pl.pallas_call(
        functools.partial(kernel, cb=cb),
        out_shape=(
            pltpu.VMEM((rows, wide), BF),
            pltpu.VMEM((wide, ff), BF),
            pltpu.VMEM((wide, ff), BF),
            pltpu.VMEM((ff, wide), BF),
            jax.ShapeDtypeStruct((rows, 2 * ff), BF),
            jax.ShapeDtypeStruct((ff, rows), BF),
        ),
        in_specs=[any_space] * 7,
        out_specs=(*[pl.BlockSpec(memory_space=pltpu.VMEM)] * 4, any_space, any_space),
        scratch_shapes=[
            pltpu.VMEM((gr // 2, half), F32),
            pltpu.VMEM((gr // 4, half), F32),
            pltpu.VMEM((gr // 8, half), F32),
            pltpu.VMEM((gr, half), BF),
            pltpu.VMEM((gr // 2, half), BF),
            pltpu.VMEM((gr // 4, half), BF),
            pltpu.VMEM((gr // 8, half), BF),
            dma((10,)),
            dma(()),
            dma((NG,)),
            dma((3,)),
            dma((3,)),
            dma((3,)),
            *[dma((3, NG))] * 3,
            *[dma((3, NG))] * 8,
            pltpu.SemaphoreType.REGULAR,
        ],
        compiler_params=pltpu.CompilerParams(
            collective_id=0, has_side_effects=True, vmem_limit_bytes=22_400_000
        ),
        name="mlp_backward",
    )(x, dy, gate, up, w_gate, w_up, w_down)
    return grads[:4]


def solution(mesh):
    tokens, columns, rows = P("dp", None), P(None, "tp"), P("tp", None)
    return jax.shard_map(
        backward,
        mesh=mesh,
        in_specs=(tokens, tokens, P("dp", "tp"), P("dp", "tp"), columns, columns, rows),
        out_specs=(tokens, P("dp", "tp"), P("dp", "tp"), P(("dp", "tp"), None)),
        check_vma=False,
    )
```

time: 194 us -> 186 us (0.959)
  Pallas kernels: 193 us -> 168 us
  local copies, waits for them, and re-layouts: 0 us -> 17.2 us
    pallas_call x2 -> x1, Pallas kernels: 193 us -> 168 us  [backward(): pl.pallas_call(functools.partial(kernel, cb=cb), out_shape=(pltpu.VMEM((r...]
    unnamed x0 -> x4, local copies, waits for them, and re-layouts: none -> 17.2 us
where the time goes in v3:
time: 186 us
  Pallas kernels  168 us (90%)
  local copies, waits for them, and re-layouts  17.2 us (9%)
    pallas_call x1, Pallas kernels, backward(): pl.pallas_call(functools.partial(kernel, cb=cb), out_shape=(pltpu.VMEM((r...  168 us
    unnamed x4, local copies, waits for them, and re-layouts  17.2 us

profile of v3, /device:TPU:0, one launch (start us, length us, event | category | flops | bytes accessed | tf_op | source)
XLA Modules:
  0.0 186.0 jit_solution(5811135351230541330)
XLA Ops:
  0.6 168.1 %mlp_backward.1 = (bf16[2048,5120]{1,0:T(8,128)(2,1)S(1)}, bf16[5120,768]{1,0:T(8,128)(2,1)S(1)}, bf16[5120,768]{1,0:T(8,128)(2,1)S(1)}, bf16[768,5120]{1,0:T(8,...) custom-call(bf16[2048,5120]{1,0:T(8,128)(2,1)} %x.1, bf16[2048,5120]{1,0:T(8,128)(2,1)} %dy.1, ...), custom_call_target="tpu_custom_call" | custom-call | tf_op jit(solution)/shard_map/mlp_backward/pallas_call | solution.py:400
  168.8 7.5 %copy.15 = bf16[2048,5120]{1,0:T(8,128)(2,1)} copy(bf16[2048,5120]{1,0:T(8,128)(2,1)S(1)} %get-tuple-element.12) | data formatting | bytes 41943040
  176.3 3.2 %copy.16 = bf16[5120,768]{1,0:T(8,128)(2,1)} copy(bf16[5120,768]{1,0:T(8,128)(2,1)S(1)} %get-tuple-element.13) | data formatting | bytes 15728640
  179.5 3.2 %copy.17 = bf16[5120,768]{1,0:T(8,128)(2,1)} copy(bf16[5120,768]{1,0:T(8,128)(2,1)S(1)} %get-tuple-element.14) | data formatting | bytes 15728640
  182.7 3.2 %copy.18 = bf16[768,5120]{1,0:T(8,128)(2,1)} copy(bf16[768,5120]{1,0:T(8,128)(2,1)S(1)} %get-tuple-element.15) | data formatting | bytes 15728640

commit v4 on v3

--- a/solution.py
+++ b/solution.py
@@ -103,8 +103,10 @@
     def c_a2(g, k):
         return remote(region(g, k, 1), region(g, k, 1), a1s.at[k, g], a1r.at[k, g], peer(stride_of(k, 0)))
 
-    def c_a3(g, k):
-        return remote(region(g, k, 0), region(g, k, 0), ds.at[k, g], dr.at[k, g], sib)
+    def c_a3(g, k, late):
+        start, size = held(k, 1)
+        rows_to = dx.at[own(g, k, size - start if late else start, size)]
+        return remote(rows_to, rows_to, ds.at[late, k, g], dr.at[late, k, g], sib)
 
     def e1(g, acc0):
         c_d2d(g).wait_recv()
@@ -171,11 +173,13 @@
         for k in range(3):
             c_a1(g, k).wait_recv()
             c_a2(g, k).start()
+        for k in range(3):
+            c_a3(g, k, 0).start()
 
     def a3(g):
         for k in range(3):
             c_a2(g, k).wait_recv()
-            c_a3(g, k).start()
+            c_a3(g, k, 1).start()
 
     def slot(s):
         @pl.when(s < 3)
@@ -192,12 +196,12 @@
         def _():
             pl.semaphore_wait(credit, 4)
 
-        for first, num, den, f in ((6, 2, 1, a3), (3, 8, 5, a2), (1, 1, 1, a1)):
+        for first, num, den, f in ((7, 9, 5, a3), (3, 3, 2, a2), (1, 1, 1, a1)):
             t = den * jnp.maximum(s - first, 0)
             g = lax.div(t, num)
             at((s >= first) & (lax.rem(t, num) < den) & (g < NG), f, g)
 
-    last_slot = 6 + 2 * (NG - 1)
+    last_slot = 7 + (9 * (NG - 1) + 4) // 5
 
     barrier = pltpu.get_barrier_semaphore()
     for to in (sib, peer(8), peer(4), peer(2)):
@@ -238,6 +242,11 @@
         def body(g, _):
             for c in rows_of(g):
                 c.wait()
+
+            @pl.when(g > 0)
+            def _():
+                for c in keep(g):
+                    c.wait()
             @pl.when(g < NG)
             def _():
                 acc0[:, pl.ds(0, ff)] = dot(dyb[...], wd[...], NT)
@@ -246,11 +255,6 @@
             gf, uf = gb[...].astype(F32), ub[...].astype(F32)
             sig = jax.nn.sigmoid(gf)
             silu = gf * sig
-
-            @pl.when(g > 0)
-            def _():
-                for c in keep(g):
-                    c.wait()
 
             d_in[:, pl.ds(0, ff)] = (d_h * uf * (sig + silu * (1 - sig))).astype(BF)
             d_in[:, pl.ds(ff, ff)] = (d_h * silu).astype(BF)
@@ -286,12 +290,12 @@
             d2d_out[...] = acc0[...].astype(BF)
 
             c_d2d(g).start()
+            reduce_events(g)
             when_first(w_mine)
             @pl.when(g < NG)
             def _():
                 acc0[...] = term(mine)
 
-            reduce_events(g)
             e1(g, acc0)
             return 0
 
@@ -385,7 +389,8 @@
             c_a0(g, k).wait_send()
             c_a1(g, k).wait_send()
             c_a2(g, k).wait_send()
-            c_a3(g, k).wait()
+            c_a3(g, k, 0).wait()
+            c_a3(g, k, 1).wait()
         return 0
 
     lax.fori_loop(0, NG, drain, 0)
@@ -424,7 +429,8 @@
             dma((3,)),
             dma((3,)),
             *[dma((3, NG))] * 3,
-            *[dma((3, NG))] * 8,
+            *[dma((3, NG))] * 6,
+            *[dma((2, 3, NG))] * 2,
             pltpu.SemaphoreType.REGULAR,
         ],
         compiler_params=pltpu.CompilerParams(

time: 186 us -> 181 us (0.973)
  Pallas kernels: 168 us -> 163 us
    pallas_call x1, Pallas kernels: 168 us -> 163 us  [backward(): pl.pallas_call(functools.partial(kernel, cb=cb), out_shape=(pltpu.VMEM((r...]
where the time goes in v4:
time: 181 us
  Pallas kernels  163 us (90%)
  local copies, waits for them, and re-layouts  17.2 us (10%)
    pallas_call x1, Pallas kernels, backward(): pl.pallas_call(functools.partial(kernel, cb=cb), out_shape=(pltpu.VMEM((r...  163 us
    unnamed x4, local copies, waits for them, and re-layouts  17.2 us

profile of v4, /device:TPU:0, one launch (start us, length us, event | category | flops | bytes accessed | tf_op | source)
XLA Modules:
  0.0 181.3 jit_solution(9829972115051435801)
XLA Ops:
  0.6 163.4 %mlp_backward.1 = (bf16[2048,5120]{1,0:T(8,128)(2,1)S(1)}, bf16[5120,768]{1,0:T(8,128)(2,1)S(1)}, bf16[5120,768]{1,0:T(8,128)(2,1)S(1)}, bf16[768,5120]{1,0:T(8,...) custom-call(bf16[2048,5120]{1,0:T(8,128)(2,1)} %x.1, bf16[2048,5120]{1,0:T(8,128)(2,1)} %dy.1, ...), custom_call_target="tpu_custom_call" | custom-call | tf_op jit(solution)/shard_map/mlp_backward/pallas_call | solution.py:405
  164.0 7.5 %copy.15 = bf16[2048,5120]{1,0:T(8,128)(2,1)} copy(bf16[2048,5120]{1,0:T(8,128)(2,1)S(1)} %get-tuple-element.12) | data formatting | bytes 41943040
  171.6 3.2 %copy.16 = bf16[5120,768]{1,0:T(8,128)(2,1)} copy(bf16[5120,768]{1,0:T(8,128)(2,1)S(1)} %get-tuple-element.13) | data formatting | bytes 15728640
  174.8 3.2 %copy.17 = bf16[5120,768]{1,0:T(8,128)(2,1)} copy(bf16[5120,768]{1,0:T(8,128)(2,1)S(1)} %get-tuple-element.14) | data formatting | bytes 15728640
  178.0 3.2 %copy.18 = bf16[768,5120]{1,0:T(8,128)(2,1)} copy(bf16[768,5120]{1,0:T(8,128)(2,1)S(1)} %get-tuple-element.15) | data formatting | bytes 15728640

commit v5 on v4

--- a/solution.py
+++ b/solution.py
@@ -76,13 +76,13 @@
         return dx[own(g, k, first + start, size)].astype(F32)
 
     def c_d2d(g):
-        return remote(d2d_out, dx.at[rows_at(g * g_rows, g_rows), pl.ds(mine, half)], d2d_s, d2d_r.at[g], sib)
+        return remote(d2d_out, dx.at[rows_at(g * g_rows, g_rows), pl.ds(mine, half)], d2d_s, d2d_r.at[lax.rem(g, 2)], sib)
 
     def c_rs(stage, g, k):
         src, send, recv = ((out1, s1, r1), (out2, s2, r2), (out3, s3, r3))[stage]
         b = bit(stride_of(k, 0))
         dst = own(g, k, *landing(g, k, stage, 1 - b if stage == 0 else b))
-        return remote(src.at[:, pl.ds(*cols[k])], dx.at[dst], send.at[k], recv.at[k, g], peer(stride_of(k, stage)))
+        return remote(src.at[:, pl.ds(*cols[k])], dx.at[dst], send.at[k], recv.at[k, lax.rem(g, 2)], peer(stride_of(k, stage)))
 
     def held(k, depth):
         start, size = 0, g_rows
@@ -95,18 +95,18 @@
         return dx.at[own(g, k, *held(k, depth))]
 
     def c_a0(g, k):
-        return remote(region(g, k, 3), region(g, k, 3), a3s.at[k, g], a3r.at[k, g], peer(stride_of(k, 2)))
+        return remote(region(g, k, 3), region(g, k, 3), a3s.at[k], a3r.at[k, g], peer(stride_of(k, 2)))
 
     def c_a1(g, k):
-        return remote(region(g, k, 2), region(g, k, 2), a2s.at[k, g], a2r.at[k, g], peer(stride_of(k, 1)))
+        return remote(region(g, k, 2), region(g, k, 2), a2s.at[k], a2r.at[k, g], peer(stride_of(k, 1)))
 
     def c_a2(g, k):
-        return remote(region(g, k, 1), region(g, k, 1), a1s.at[k, g], a1r.at[k, g], peer(stride_of(k, 0)))
+        return remote(region(g, k, 1), region(g, k, 1), a1s.at[k], a1r.at[k, g], peer(stride_of(k, 0)))
 
     def c_a3(g, k, late):
         start, size = held(k, 1)
         rows_to = dx.at[own(g, k, size - start if late else start, size)]
-        return remote(rows_to, rows_to, ds.at[late, k, g], dr.at[late, k, g], sib)
+        return remote(rows_to, rows_to, ds.at[k], dr.at[k], sib)
 
     def e1(g, acc0):
         c_d2d(g).wait_recv()
@@ -384,16 +384,10 @@
             c_rs(stage, NG - 1, k).wait_send()
     c_d2d(NG - 1).wait_send()
 
-    def drain(g, _):
-        for k in range(3):
-            c_a0(g, k).wait_send()
-            c_a1(g, k).wait_send()
-            c_a2(g, k).wait_send()
-            c_a3(g, k, 0).wait()
-            c_a3(g, k, 1).wait()
-        return 0
-
-    lax.fori_loop(0, NG, drain, 0)
+    for k in range(3):
+        for sem, part in ((a3s, 8), (a2s, 4), (a1s, 2), (ds, 1), (dr, 1)):
+            whole = dx.at[pl.ds(0, rows // part), pl.ds(*cols[k])]
+            pltpu.make_async_copy(whole, whole, sem.at[k]).wait()
 
 
 def backward(x, dy, gate, up, w_gate, w_up, w_down, *, cb=256):
@@ -424,13 +418,13 @@
             pltpu.VMEM((gr // 8, half), BF),
             dma((10,)),
             dma(()),
-            dma((NG,)),
+            dma((2,)),
             dma((3,)),
             dma((3,)),
             dma((3,)),
-            *[dma((3, NG))] * 3,
-            *[dma((3, NG))] * 6,
-            *[dma((2, 3, NG))] * 2,
+            *[dma((3, 2))] * 3,
+            *[dma((3,)), dma((3, NG))] * 3,
+            *[dma((3,))] * 2,
             pltpu.SemaphoreType.REGULAR,
         ],
         compiler_params=pltpu.CompilerParams(

time: 181 us -> 180 us (level)
  no operation moved by 1% of the time
where the time goes in v5:
time: 180 us
  Pallas kernels  162 us (90%)
  local copies, waits for them, and re-layouts  17.2 us (10%)
    pallas_call x1, Pallas kernels, backward(): pl.pallas_call(functools.partial(kernel, cb=cb), out_shape=(pltpu.VMEM((r...  162 us
    unnamed x4, local copies, waits for them, and re-layouts  17.2 us

profile of v5, /device:TPU:0, one launch (start us, length us, event | category | flops | bytes accessed | tf_op | source)
XLA Modules:
  0.0 180.0 jit_solution(6130584712364768918)
XLA Ops:
  0.6 162.1 %mlp_backward.1 = (bf16[2048,5120]{1,0:T(8,128)(2,1)S(1)}, bf16[5120,768]{1,0:T(8,128)(2,1)S(1)}, bf16[5120,768]{1,0:T(8,128)(2,1)S(1)}, bf16[768,5120]{1,0:T(8,...) custom-call(bf16[2048,5120]{1,0:T(8,128)(2,1)} %x.1, bf16[2048,5120]{1,0:T(8,128)(2,1)} %dy.1, ...), custom_call_target="tpu_custom_call" | custom-call | tf_op jit(solution)/shard_map/mlp_backward/pallas_call | solution.py:399
  162.7 7.5 %copy.15 = bf16[2048,5120]{1,0:T(8,128)(2,1)} copy(bf16[2048,5120]{1,0:T(8,128)(2,1)S(1)} %get-tuple-element.12) | data formatting | bytes 41943040
  170.3 3.2 %copy.16 = bf16[5120,768]{1,0:T(8,128)(2,1)} copy(bf16[5120,768]{1,0:T(8,128)(2,1)S(1)} %get-tuple-element.13) | data formatting | bytes 15728640
  173.5 3.2 %copy.17 = bf16[5120,768]{1,0:T(8,128)(2,1)} copy(bf16[5120,768]{1,0:T(8,128)(2,1)S(1)} %get-tuple-element.14) | data formatting | bytes 15728640
  176.7 3.2 %copy.18 = bf16[768,5120]{1,0:T(8,128)(2,1)} copy(bf16[768,5120]{1,0:T(8,128)(2,1)S(1)} %get-tuple-element.15) | data formatting | bytes 15728640

commit v6 on v5

--- a/solution.py
+++ b/solution.py
@@ -14,6 +14,7 @@
 NN = (((1,), (0,)), ((), ()))
 NG = 8
 ORDERS = ((8, 4, 2), (4, 2, 8), (2, 8, 4))
+SECOND = ((2, 4, 8), (8, 2, 4), (4, 8, 2))
 
 
 def dot(a, b, dims):
@@ -45,7 +46,7 @@
     other = pl.multiple_of((1 - core) * half, 128)
 
     def stride_of(k, stage):
-        first, second = ORDERS[k][stage], ORDERS[(k + 1) % 3][stage]
+        first, second = ORDERS[k][stage], SECOND[k][stage]
         return first + core * (second - first)
 
     def bit(stride):
@@ -75,8 +76,9 @@
         first, _ = landing(g, k, stage, bit(stride_of(k, 0)))
         return dx[own(g, k, first + start, size)].astype(F32)
 
-    def c_d2d(g):
-        return remote(d2d_out, dx.at[rows_at(g * g_rows, g_rows), pl.ds(mine, half)], d2d_s, d2d_r.at[lax.rem(g, 2)], sib)
+    def c_d2d(g, k):
+        dst = dx.at[own(g, k, 0, g_rows)]
+        return remote(d2d_out.at[:, pl.ds(*cols[k])], dst, d2d_s.at[k], d2d_r.at[k, lax.rem(g, 2)], sib)
 
     def c_rs(stage, g, k):
         src, send, recv = ((out1, s1, r1), (out2, s2, r2), (out3, s3, r3))[stage]
@@ -109,7 +111,6 @@
         return remote(rows_to, rows_to, ds.at[k], dr.at[k], sib)
 
     def e1(g, acc0):
-        c_d2d(g).wait_recv()
         h = g_rows // 2
 
         def chip_sum(k, start):
@@ -117,6 +118,7 @@
             return acc0[rows_at(start, h), pl.ds(*cols[k])] + theirs.astype(F32)
 
         for k in range(3):
+            c_d2d(g, k).wait_recv()
 
             @pl.when(g > 0)
             def _():
@@ -153,6 +155,10 @@
     def a0(g):
         for k in range(3):
             c_a0(g, k).start()
+
+    def early(g, _):
+        a0(g)
+        return 0
 
     def at(cond, f, g):
         @pl.when(cond)
@@ -187,6 +193,10 @@
             reduce_events(NG + s)
             at(s >= 0, a0, NG + s - 3)
 
+            @pl.when(s == 0)
+            def _():
+                lax.fori_loop(2, NG - 3, early, 0)
+
         @pl.when(s == 2)
         def _():
             for to in (sib, peer(8), peer(4), peer(2)):
@@ -196,12 +206,12 @@
         def _():
             pl.semaphore_wait(credit, 4)
 
-        for first, num, den, f in ((7, 9, 5, a3), (3, 3, 2, a2), (1, 1, 1, a1)):
+        for first, num, den, f in ((9, 8, 5, a3), (3, 3, 2, a2), (1, 1, 1, a1)):
             t = den * jnp.maximum(s - first, 0)
             g = lax.div(t, num)
             at((s >= first) & (lax.rem(t, num) < den) & (g < NG), f, g)
 
-    last_slot = 7 + (9 * (NG - 1) + 4) // 5
+    last_slot = 9 + (8 * (NG - 1) + 4) // 5
 
     barrier = pltpu.get_barrier_semaphore()
     for to in (sib, peer(8), peer(4), peer(2)):
@@ -281,7 +291,8 @@
 
             @pl.when(g > 0)
             def _():
-                c_d2d(g).wait_send()
+                for k in range(3):
+                    c_d2d(g, k).wait_send()
 
             @pl.when(g < NG)
             def _():
@@ -289,7 +300,8 @@
 
             d2d_out[...] = acc0[...].astype(BF)
 
-            c_d2d(g).start()
+            for k in range(3):
+                c_d2d(g, k).start()
             reduce_events(g)
             when_first(w_mine)
             @pl.when(g < NG)
@@ -328,11 +340,7 @@
         for c in loads(0, 0):
             c.start()
 
-        def early(g, _):
-            a0(g)
-            return 0
-
-        lax.fori_loop(0, NG - 3, early, 0)
+        lax.fori_loop(0, 2, early, 0)
         for c in again:
             c.wait()
 
@@ -382,7 +390,7 @@
     for k in range(3):
         for stage in range(3):
             c_rs(stage, NG - 1, k).wait_send()
-    c_d2d(NG - 1).wait_send()
+        c_d2d(NG - 1, k).wait_send()
 
     for k in range(3):
         for sem, part in ((a3s, 8), (a2s, 4), (a1s, 2), (ds, 1), (dr, 1)):
@@ -417,8 +425,8 @@
             pltpu.VMEM((gr // 4, half), BF),
             pltpu.VMEM((gr // 8, half), BF),
             dma((10,)),
-            dma(()),
-            dma((2,)),
+            dma((3,)),
+            dma((3, 2)),
             dma((3,)),
             dma((3,)),
             dma((3,)),

time: 180 us -> 177 us (0.983)
  Pallas kernels: 162 us -> 159 us
    pallas_call x1, Pallas kernels: 162 us -> 159 us  [backward(): pl.pallas_call(functools.partial(kernel, cb=cb), out_shape=(pltpu.VMEM((r...]
where the time goes in v6:
time: 177 us
  Pallas kernels  159 us (90%)
  local copies, waits for them, and re-layouts  17.2 us (10%)
    pallas_call x1, Pallas kernels, backward(): pl.pallas_call(functools.partial(kernel, cb=cb), out_shape=(pltpu.VMEM((r...  159 us
    unnamed x4, local copies, waits for them, and re-layouts  17.2 us

profile of v6, /device:TPU:0, one launch (start us, length us, event | category | flops | bytes accessed | tf_op | source)
XLA Modules:
  0.0 176.6 jit_solution(1789292830207958654)
XLA Ops:
  0.6 158.8 %mlp_backward.1 = (bf16[2048,5120]{1,0:T(8,128)(2,1)S(1)}, bf16[5120,768]{1,0:T(8,128)(2,1)S(1)}, bf16[5120,768]{1,0:T(8,128)(2,1)S(1)}, bf16[768,5120]{1,0:T(8,...) custom-call(bf16[2048,5120]{1,0:T(8,128)(2,1)} %x.1, bf16[2048,5120]{1,0:T(8,128)(2,1)} %dy.1, ...), custom_call_target="tpu_custom_call" | custom-call | tf_op jit(solution)/shard_map/mlp_backward/pallas_call | solution.py:407
  159.4 7.5 %copy.15 = bf16[2048,5120]{1,0:T(8,128)(2,1)} copy(bf16[2048,5120]{1,0:T(8,128)(2,1)S(1)} %get-tuple-element.12) | data formatting | bytes 41943040
  167.0 3.2 %copy.16 = bf16[5120,768]{1,0:T(8,128)(2,1)} copy(bf16[5120,768]{1,0:T(8,128)(2,1)S(1)} %get-tuple-element.13) | data formatting | bytes 15728640
  170.2 3.2 %copy.17 = bf16[5120,768]{1,0:T(8,128)(2,1)} copy(bf16[5120,768]{1,0:T(8,128)(2,1)S(1)} %get-tuple-element.14) | data formatting | bytes 15728640
  173.4 3.2 %copy.18 = bf16[768,5120]{1,0:T(8,128)(2,1)} copy(bf16[768,5120]{1,0:T(8,128)(2,1)S(1)} %get-tuple-element.15) | data formatting | bytes 15728640

commit v7 on v6

--- a/solution.py
+++ b/solution.py
@@ -327,9 +327,6 @@
 
     def second_phase(d_all, hid_t, xb, yb):
         again = (pltpu.make_async_copy(d_kept, d_all, load.at[8]), pltpu.make_async_copy(hid_kept, hid_t, load.at[9]))
-        for c in again:
-            c.start()
-
         def loads(i, b):
             c = rows_at(i * cb, cb)
             return (
@@ -337,12 +334,12 @@
                 pltpu.make_async_copy(dy.at[:, c], yb.at[b], load.at[2 + b]),
             )
 
-        for c in loads(0, 0):
+        first = loads(0, 0)
+        for c in (first[0], again[0], first[1], again[1]):
             c.start()
 
         lax.fori_loop(0, 2, early, 0)
-        for c in again:
-            c.wait()
+        again[0].wait()
 
         def body(i, _):
             b = lax.rem(i, 2)
@@ -363,6 +360,10 @@
                 dw_up[c, :] = both[:, ff:]
 
             into[1].wait()
+
+            @pl.when(i == 0)
+            def _():
+                again[1].wait()
 
             @pl.when(i < steps)
             def _():

time: 177 us -> 177 us (level)
  no operation moved by 1% of the time
where the time goes in v7:
time: 177 us
  Pallas kernels  159 us (90%)
  local copies, waits for them, and re-layouts  17.2 us (10%)
    pallas_call x1, Pallas kernels, backward(): pl.pallas_call(functools.partial(kernel, cb=cb), out_shape=(pltpu.VMEM((r...  159 us
    unnamed x4, local copies, waits for them, and re-layouts  17.2 us

profile of v7, /device:TPU:0, one launch (start us, length us, event | category | flops | bytes accessed | tf_op | source)
XLA Modules:
  0.0 176.6 jit_solution(736256039707233801)
XLA Ops:
  0.6 158.8 %mlp_backward.1 = (bf16[2048,5120]{1,0:T(8,128)(2,1)S(1)}, bf16[5120,768]{1,0:T(8,128)(2,1)S(1)}, bf16[5120,768]{1,0:T(8,128)(2,1)S(1)}, bf16[768,5120]{1,0:T(8,...) custom-call(bf16[2048,5120]{1,0:T(8,128)(2,1)} %x.1, bf16[2048,5120]{1,0:T(8,128)(2,1)} %dy.1, ...), custom_call_target="tpu_custom_call" | custom-call | tf_op jit(solution)/shard_map/mlp_backward/pallas_call | solution.py:408
  159.4 7.5 %copy.15 = bf16[2048,5120]{1,0:T(8,128)(2,1)} copy(bf16[2048,5120]{1,0:T(8,128)(2,1)S(1)} %get-tuple-element.12) | data formatting | bytes 41943040
  167.0 3.2 %copy.16 = bf16[5120,768]{1,0:T(8,128)(2,1)} copy(bf16[5120,768]{1,0:T(8,128)(2,1)S(1)} %get-tuple-element.13) | data formatting | bytes 15728640
  170.2 3.2 %copy.17 = bf16[5120,768]{1,0:T(8,128)(2,1)} copy(bf16[5120,768]{1,0:T(8,128)(2,1)S(1)} %get-tuple-element.14) | data formatting | bytes 15728640
  173.4 3.2 %copy.18 = bf16[768,5120]{1,0:T(8,128)(2,1)} copy(bf16[768,5120]{1,0:T(8,128)(2,1)S(1)} %get-tuple-element.15) | data formatting | bytes 15728640
